TPU v7x, 32 devices: a whole 2x2x4 slice. The times are simulated.
32 devices in a mesh: replica: 4 (over z), tp: 8 (over y, x, core).
Axes of the slice: x: 2, y: 2, z: 4, core: 2. Of those that a mesh axis runs over, the one named last changes fastest.
Arguments:
- hidden: bfloat16 [256, 8192], P(('replica', 'tp')), may hold values from -64 to 64
- head: bfloat16 [152064, 8192], P(('replica', 'tp'))
- token_ids: int32 [256], replicated, may hold values from 0 to 152063
Outputs:
- logprob: float32 [256], P(('replica', 'tp'))
All inputs are finite; a program needn't handle non-finite values.
Results may differ from a plain program's by a relative error of at most 0.0003.
Values may be sent and summed in bfloat16 or wider, within the bound.
A program may use at most 128 MiB of HBM per device.

v0:
```python
import jax
import jax.numpy as jnp
from jax import lax
from jax.sharding import PartitionSpec as P


def shards(hidden, head, token_ids):
    device_count = lax.axis_size("replica") * lax.axis_size("tp")
    per_device = hidden.shape[0]
    local_vocab = head.shape[0]
    position = lax.axis_index(("replica", "tp"))
    columns = position * local_vocab + jnp.arange(local_vocab, dtype=jnp.int32)
    gathered = lax.all_gather(hidden, ("replica", "tp"), axis=0, tiled=True)
    logits = lax.dot_general(
        gathered, head, (((1,), (1,)), ((), ())), preferred_element_type=jnp.float32
    )
    row_top = jnp.max(logits, axis=1)
    row_total = jnp.sum(jnp.exp(logits - row_top[:, None]), axis=1)
    row_picked = jnp.sum(jnp.where(columns[None, :] == token_ids[:, None], logits, 0.0), axis=1)
    stats = (row_top, row_total, row_picked)
    row_top, row_total, row_picked = stats
    shaped = (
        row_top.reshape(device_count, per_device),
        row_total.reshape(device_count, per_device),
        row_picked.reshape(device_count, per_device),
    )
    arrived = (
        lax.all_to_all(shaped[0], ("replica", "tp"), split_axis=0, concat_axis=0, tiled=True),
        lax.all_to_all(shaped[1], ("replica", "tp"), split_axis=0, concat_axis=0, tiled=True),
        lax.all_to_all(shaped[2], ("replica", "tp"), split_axis=0, concat_axis=0, tiled=True),
    )
    final_top = jnp.max(arrived[0], axis=0)
    final_total = jnp.sum(arrived[1] * jnp.exp(arrived[0] - final_top[None, :]), axis=0)
    final_picked = jnp.sum(arrived[2], axis=0)
    return final_picked - final_top - jnp.log(final_total)


def solution(mesh):
    in_specs = (P(("replica", "tp"), None), P(("replica", "tp"), None), P())
    out_specs = P(("replica", "tp"))
    return jax.shard_map(shards, mesh=mesh, in_specs=in_specs, out_specs=out_specs, check_vma=False)
```

profile of v0, /device:TPU:0, one launch (start us, length us, event | category | flops | bytes accessed | tf_op | source)
XLA Modules:
  0.0 146.2 jit_solution(7988030538817095933)
XLA Ops:
  6.5 0.0 all-gather.2.cloned.1.call-start
  6.5 0.7 all-gather.2.cloned.1.call-update
  7.3 0.0 copy-start
  7.3 67.4 %all-gather.2.cloned.1.call-done = bf16[256,8192]{1,0:T(8,128)(2,1)} async-done(((bf16[8,8192]{1,0:T(8,128)(2,1)}), bf16[256,8192]{1,0:T(8,128)(2,1)}) %all-gather.2.cloned.1.call-update) | async-done | bytes 4194320 | tf_op jit(solution)/shard_map/all_gather | solution.py:13
  74.7 32.4 %fusion = (f32[256]{0:T(256)S(1)}, f32[256,4752]{0,1:T(8,128)}) fusion(bf16[256,8192]{1,0:T(8,128)(2,1)} %all-gather.2.cloned.1.call-done, bf16[4752,8192]{1,0:T(8,128)(2,1)} %param.4), kind=kOutput, calls=%fused_computation.5 | convolution fusion | flops 19932549120 | bytes 86918144 | tf_op jit(solution)/shard_map/dot_general | solution.py:14
  107.0 0.7 all_to_all.24
  107.7 3.4 %all-to-all-start.1 = ((f32[32,1,8]{2,1,0:T(1,128)}), f32[32,1,8]{2,1,0:T(1,128)S(1)}, u32[]{:S(2)}, u32[]{:S(2)}) async-start(f32[32,1,8]{2,1,0:T(1,128)} %bitcast.1), calls=%async_computation.1 | async-start | bytes 32768 | tf_op jit(solution)/shard_map/all_to_all | solution.py:28
  111.1 0.0 copy-done
  111.1 4.3 %select_reduce_fusion = (f32[256]{0:T(256)S(1)}, f32[256]{0:T(256)S(1)}) fusion(f32[256,4752]{0,1:T(8,128)} %get-tuple-element.8, s32[256]{0:T(256)S(1)} %copy-done, s32[4752]{0:T(1024)S(1)} %iota_add_fusion, f32[256]{0:T(256)S(1)} %get-tuple-element.7), kind=kLoop, calls=%fused_computation.1 | loop fusion | flops 6082048 | bytes 4889152 | tf_op jit(solution)/shard_map/reduce_sum | solution.py:19
  115.4 0.7 all_to_all.26
  116.1 2.2 %all-to-all-done.1 = f32[32,1,8]{2,1,0:T(1,128)S(1)} async-done(((f32[32,1,8]{2,1,0:T(1,128)}), f32[32,1,8]{2,1,0:T(1,128)S(1)}, u32[]{:S(2)}, u32[]{:S(2)}) %all-to-all-start.1) | async-done | bytes 1056 | tf_op jit(solution)/shard_map/all_to_all | solution.py:28
  118.3 3.6 %all-to-all-start.2 = ((f32[32,1,8]{2,1,0:T(1,128)}), f32[32,1,8]{2,1,0:T(1,128)S(1)}, u32[]{:S(2)}, u32[]{:S(2)}) async-start(f32[32,1,8]{2,1,0:T(1,128)} %bitcast.2), calls=%async_computation.2 | async-start | bytes 32768 | tf_op jit(solution)/shard_map/all_to_all | solution.py:29
  121.9 0.7 all_to_all.22
  122.6 0.1 reduce_max.19
  122.7 6.4 %all-to-all-done.2 = f32[32,1,8]{2,1,0:T(1,128)S(1)} async-done(((f32[32,1,8]{2,1,0:T(1,128)}), f32[32,1,8]{2,1,0:T(1,128)S(1)}, u32[]{:S(2)}, u32[]{:S(2)}) %all-to-all-start.2) | async-done | bytes 1056 | tf_op jit(solution)/shard_map/all_to_all | solution.py:29
  129.1 2.5 %all-to-all-start = ((f32[32,1,8]{2,1,0:T(1,128)}), f32[32,1,8]{2,1,0:T(1,128)S(1)}, u32[]{:S(2)}, u32[]{:S(2)}) async-start(f32[32,1,8]{2,1,0:T(1,128)} %bitcast), calls=%async_computation | async-start | bytes 32768 | tf_op jit(solution)/shard_map/all_to_all | solution.py:30
  131.6 7.1 %all-to-all-done = f32[32,1,8]{2,1,0:T(1,128)S(1)} async-done(((f32[32,1,8]{2,1,0:T(1,128)}), f32[32,1,8]{2,1,0:T(1,128)S(1)}, u32[]{:S(2)}, u32[]{:S(2)}) %all-to-all-start) | async-done | bytes 1056 | tf_op jit(solution)/shard_map/all_to_all | solution.py:30
  138.8 0.1 reduce_sum.37
  138.8 0.5 log_subtract_fusion
  (2 shorter events, 0.0 us)
Async XLA Ops:
  6.5 68.1 %all-gather.2.cloned.1.call-start = ((), (), s32[]{:S(2)}) async-start(), calls=%async_computation.3 | async-start | bytes 4325376 | tf_op jit(solution)/shard_map/all_gather | solution.py:13
  7.3 103.8 %copy-start = (s32[256]{0:T(256)S(1)}, s32[256]{0:T(256)}, u32[]{:S(2)}) copy-start(s32[256]{0:T(256)} %param.5) | copy-start | bytes 3076
  107.7 10.6 %all-to-all-start.1 = ((f32[32,1,8]{2,1,0:T(1,128)}), f32[32,1,8]{2,1,0:T(1,128)S(1)}, u32[]{:S(2)}, u32[]{:S(2)}) async-start(f32[32,1,8]{2,1,0:T(1,128)} %bitcast.1), calls=%async_computation.1 | async-start | bytes 32768 | tf_op jit(solution)/shard_map/all_to_all | solution.py:28
  118.3 10.8 %all-to-all-start.2 = ((f32[32,1,8]{2,1,0:T(1,128)}), f32[32,1,8]{2,1,0:T(1,128)S(1)}, u32[]{:S(2)}, u32[]{:S(2)}) async-start(f32[32,1,8]{2,1,0:T(1,128)} %bitcast.2), calls=%async_computation.2 | async-start | bytes 32768 | tf_op jit(solution)/shard_map/all_to_all | solution.py:29
  129.1 9.7 %all-to-all-start = ((f32[32,1,8]{2,1,0:T(1,128)}), f32[32,1,8]{2,1,0:T(1,128)S(1)}, u32[]{:S(2)}, u32[]{:S(2)}) async-start(f32[32,1,8]{2,1,0:T(1,128)} %bitcast), calls=%async_computation | async-start | bytes 32768 | tf_op jit(solution)/shard_map/all_to_all | solution.py:30
Sparse Core Ops, SparseCore 0:
  10.2 64.4 all-gather.1
where the time goes:
time: 147 us; the launch traced here: 146 us
  waiting for transfers between devices  83.9 us (57%)
  matrix products  32.4 us (22%)
  between operations  13.4 us (9%)
  starting transfers between devices  9.48 us (6%)
  other arithmetic  4.92 us (3%)
  local copies, waits for them, and re-layouts  2.07 us (1%)
    all_gather x1, waiting for transfers between devices, shards(): gathered = lax.all_gather(hidden, ('replica', 'tp'), axis=0, tiled=True)  67.4 us
    dot_general x1, matrix products, shards(): lax.dot_general(gathered, head, (((1,), (1,)), ((), ())), preferred_eleme...  32.4 us
    all_to_all x1, waiting for transfers between devices, shards(): lax.all_to_all(shaped[2], ('replica', 'tp'), split_axis=0, concat_axis=0,...  7.15 us
    all_to_all x1, waiting for transfers between devices, shards(): lax.all_to_all(shaped[1], ('replica', 'tp'), split_axis=0, concat_axis=0,...  6.43 us
    reduce_sum x1, other arithmetic, shards(): jnp.sum(jnp.where(columns[None, :] == token_ids[:, None], logits, 0.0), a...  4.26 us
    all_to_all x1, starting transfers between devices, shards(): lax.all_to_all(shaped[1], ('replica', 'tp'), split_axis=0, concat_axis=0,...  3.62 us
    all_to_all x1, starting transfers between devices, shards(): lax.all_to_all(shaped[0], ('replica', 'tp'), split_axis=0, concat_axis=0,...  3.38 us
  transfers between devices with their start and end apart: 4, of which 4 were waited for; matrix products, arithmetic and copies ran while one was open for 3% of the time, Pallas kernels for 0%

commit v1 on v0

v1 whole, which is shorter than its diff:
```python
import functools

import jax
import jax.numpy as jnp
from jax import lax
from jax.experimental import pallas as pl
from jax.experimental.pallas import tpu as pltpu
from jax.sharding import PartitionSpec as P

MESH = pl.DeviceIdType.MESH
SLICES = 4
PIECES = 2 * SLICES
VMEM = 66_000_000


def chunk_rows(rows, limit):
    return max((r for r in range(8, limit + 1, 8) if rows % r == 0), default=rows)


def split_axis(size):
    return (size // 4, 2, 2) if size % 4 == 0 else (size, 1, 1)


def kernel(dims, rows, slots, tokens_ref, hidden_ref, head_ref, out_ref, ring, acc, gathered, hid,
           stats, sent, arrived, ring_sem, own_sem, gsend, grecv, ssend, srecv):
    z_n, y_n, x_n, c_n = dims
    tp_n = y_n * x_n * c_n
    devices = z_n * tp_n
    z = lax.axis_index("replica")
    t = lax.axis_index("tp")
    me = z * tp_n + t
    y, x, c = t // (x_n * c_n), (t // c_n) % x_n, t % c_n
    at = (z, y, x, c)
    per_device, depth = hidden_ref.shape
    local_vocab = head_ref.shape[0]
    seqs = hid.shape[0]
    piece_k, slice_k = depth // PIECES, depth // SLICES
    chunks = local_vocab // rows
    blocks = chunks * SLICES

    def fetch(i, slot):
        s, k = i // chunks, i % chunks
        return pltpu.make_async_copy(
            head_ref.at[pl.ds(pl.multiple_of(k * rows, 8), rows), pl.ds(pl.multiple_of(s * slice_k, 128), slice_k)],
            ring.at[slot], ring_sem.at[slot])

    def own(p):
        return pltpu.make_async_copy(
            hidden_ref.at[:, pl.ds(p * piece_k, piece_k)], gathered.at[p, z, y, x, c], own_sem.at[p])

    for p in range(PIECES):
        own(p).start()

    @pl.loop(0, slots)
    def _(i):
        fetch(i, i).start()

    barrier = pltpu.get_barrier_semaphore()

    @pl.loop(1, devices)
    def _(k):
        d = (me + k) % devices
        pl.semaphore_signal(barrier, inc=1, device_id=(d // tp_n, d % tp_n), device_id_type=MESH)

    pl.semaphore_wait(barrier, devices - 1)

    def order(p):
        return (0, 1, 2, 3) if p % 2 == 0 else (0, 2, 1, 3)

    def copy(p, phase, k, incoming=False):
        path = order(p)
        axis = path[phase]
        n = dims[axis]
        there = list(at)
        there[axis] = (at[axis] + k) % n
        mine = at[axis] if not incoming else (at[axis] + n - k) % n
        index = [p]
        for a in range(4):
            if a in path[:phase]:
                index.append(slice(None))
            elif a == axis:
                index.append(mine)
            else:
                index.append(at[a])
        ref = gathered.at[tuple(index)]
        device = (there[0], (there[1] * x_n + there[2]) * c_n + there[3])
        return pltpu.make_async_remote_copy(
            src_ref=ref, dst_ref=ref, send_sem=gsend.at[p, phase, k - 1], recv_sem=grecv.at[p, phase, k - 1],
            device_id=device, device_id_type=MESH)

    def hops(p, phase):
        return range(1, dims[order(p)[phase]])

    def arrive(p, phase):
        for k in hops(p, phase):
            copy(p, phase, k, incoming=True).wait_recv()

    def step(s, phase):
        for p in (2 * s, 2 * s + 1):
            if phase == 0:
                own(p).wait()
            else:
                arrive(p, phase - 1)
            for k in hops(p, phase):
                copy(p, phase, k).start()

    def finish(s):
        for p in (2 * s, 2 * s + 1):
            arrive(p, 3)
            block = gathered[p].astype(jnp.float32).reshape(seqs, piece_k)
            hid[:, p * piece_k:(p + 1) * piece_k] = block.astype(jnp.bfloat16)

    stats[0:1, :] = jnp.full((1, seqs), -jnp.inf, jnp.float32)
    stats[1:3, :] = jnp.zeros((2, seqs), jnp.float32)

    def compute(s, low, high):
        def body(k, carry):
            i = s * chunks + k
            slot = i % slots
            fetch(i, slot).wait()
            part = lax.dot_general(ring[slot], hid[:, s * slice_k:(s + 1) * slice_k], (((1,), (1,)), ((), ())),
                                   preferred_element_type=jnp.float32)
            place = pl.ds(pl.multiple_of(k * rows, 8), rows)
            if s == 0:
                acc[place, :] = part
            elif s < SLICES - 1:
                acc[place, :] += part
            else:
                logits = acc[place, :] + part
                top = stats[0:1, :]
                new_top = jnp.maximum(top, jnp.max(logits, axis=0, keepdims=True))
                column = lax.broadcasted_iota(jnp.int32, logits.shape, 0) + (me * local_vocab + k * rows)
                hit = jnp.where(column == tokens_ref[...], logits, 0.0)
                total = jnp.sum(jnp.exp(logits - new_top), axis=0, keepdims=True)
                stats[0:1, :] = new_top
                stats[1:2, :] = stats[1:2, :] * jnp.exp(top - new_top) + total
                stats[2:3, :] += jnp.sum(hit, axis=0, keepdims=True)

            @pl.when(i + slots < blocks)
            def _():
                fetch(i + slots, slot).start()
            return carry
        lax.fori_loop(low, high, body, 0)

    for s in range(SLICES):
        step(s, 0)
    todo = [(s, w - s + 1) for w in range(3 + SLICES) for s in range(SLICES) if 1 <= w - s + 1 <= 3]
    first = todo.index((0, 3)) + 1
    for s, phase in todo[:first]:
        step(s, phase)
    rest = todo[first:]
    parts = max(1, min(chunks, len(rest)))
    edges = [chunks * j // parts for j in range(parts + 1)]
    finish(0)
    for j in range(parts):
        for s, phase in rest[len(rest) * j // parts:len(rest) * (j + 1) // parts]:
            step(s, phase)
        compute(0, edges[j], edges[j + 1])
    for s in range(1, SLICES):
        finish(s)
        compute(s, 0, chunks)

    line = lax.broadcasted_iota(jnp.int32, (128, seqs), 0)
    table = jnp.where(line == 0, stats[0:1, :], jnp.where(line == 1, stats[1:2, :], stats[2:3, :]))
    sent[...] = table.T.reshape(devices, per_device, 128)
    arrived[pl.ds(me, 1)] = sent[pl.ds(me, 1)]

    def result(k, incoming=False):
        d = (me + k) % devices
        origin = (me + devices - k) % devices if incoming else me
        return pltpu.make_async_remote_copy(
            src_ref=sent.at[d], dst_ref=arrived.at[origin], send_sem=ssend.at[k], recv_sem=srecv.at[k],
            device_id=(d // tp_n, d % tp_n), device_id_type=MESH)

    @pl.loop(1, devices)
    def _(k):
        result(k).start()

    for p in range(PIECES):
        for phase in range(4):
            for k in hops(p, phase):
                copy(p, phase, k).wait_send()

    @pl.loop(1, devices)
    def _(k):
        result(k, incoming=True).wait_recv()
        result(k).wait_send()

    table = arrived[...]
    tops, totals, picked = table[:, :, 0:1], table[:, :, 1:2], table[:, :, 2:3]
    top = jnp.max(tops, axis=0)
    total = jnp.sum(totals * jnp.exp(tops - top[None]), axis=0)
    value = jnp.sum(picked, axis=0) - top - jnp.log(total)
    out_ref[...] = jnp.broadcast_to(value, out_ref.shape)


def shards(z_n, tp_n, hidden, head, token_ids):
    dims = (z_n,) + split_axis(tp_n)
    devices = z_n * tp_n
    per_device, depth = hidden.shape
    seqs = per_device * devices
    rows = chunk_rows(head.shape[0], 528)
    blocks = head.shape[0] // rows * SLICES
    block_bytes = rows * depth // SLICES * 2
    fixed = head.shape[0] * seqs * 4 + 2 * seqs * depth * 2 + 2 * rows * seqs * 4 + 3 * 2**20
    slots = max(2, min(blocks, (VMEM - fixed) // block_bytes))
    hop_n = max(max(dims) - 1, 1)
    out = pl.pallas_call(
        functools.partial(kernel, dims, rows, slots),
        out_shape=jax.ShapeDtypeStruct((per_device, 128), jnp.float32),
        in_specs=[pl.BlockSpec(memory_space=pltpu.VMEM), pl.BlockSpec(memory_space=pltpu.HBM),
                  pl.BlockSpec(memory_space=pltpu.HBM)],
        out_specs=pl.BlockSpec(memory_space=pltpu.VMEM),
        scratch_shapes=[
            pltpu.VMEM((slots, rows, depth // SLICES), jnp.bfloat16),
            pltpu.VMEM((head.shape[0], seqs), jnp.float32),
            pltpu.VMEM((PIECES,) + dims + (per_device, depth // PIECES), jnp.bfloat16),
            pltpu.VMEM((seqs, depth), jnp.bfloat16),
            pltpu.VMEM((8, seqs), jnp.float32),
            pltpu.VMEM((devices, per_device, 128), jnp.float32),
            pltpu.VMEM((devices, per_device, 128), jnp.float32),
            pltpu.SemaphoreType.DMA((slots,)),
            pltpu.SemaphoreType.DMA((PIECES,)),
            pltpu.SemaphoreType.DMA((PIECES, 4, hop_n)),
            pltpu.SemaphoreType.DMA((PIECES, 4, hop_n)),
            pltpu.SemaphoreType.DMA((devices,)),
            pltpu.SemaphoreType.DMA((devices,)),
        ],
        compiler_params=pltpu.CompilerParams(
            collective_id=0, has_side_effects=True, vmem_limit_bytes=67_000_000),
    )(token_ids.reshape(1, seqs), hidden, head)
    return out[:, 0]


def solution(mesh):
    in_specs = (P(("replica", "tp"), None), P(("replica", "tp"), None), P())
    body = functools.partial(shards, mesh.shape["replica"], mesh.shape["tp"])
    return jax.shard_map(body, mesh=mesh, in_specs=in_specs, out_specs=P(("replica", "tp")), check_vma=False)
```

time: 147 us -> 72.7 us (0.49)
  waiting for transfers between devices: 83.9 us -> 0 us
  Pallas kernels: 0 us -> 71.2 us
  matrix products: 32.4 us -> 0 us
  between operations: 13.4 us -> 0.01 us
  starting transfers between devices: 9.48 us -> 0 us
  other arithmetic: 4.92 us -> 0 us
    pallas_call x0 -> x1, Pallas kernels: none -> 71.2 us  [shards(): pl.pallas_call(functools.partial(kernel, dims, rows, slots), out_shape=ja...]
    all_gather x1 -> x0, waiting for transfers between devices: 67.4 us -> none  [shards(): gathered = lax.all_gather(hidden, ('replica', 'tp'), axis=0, tiled=True)]
    dot_general x1 -> x0, matrix products: 32.4 us -> none  [shards(): lax.dot_general(gathered, head, (((1,), (1,)), ((), ())), preferred_eleme...]
    all_to_all x3 -> x0, waiting for transfers between devices: 15.8 us -> none  [the longest x1 7.15 us: shards(): lax.all_to_all(shaped[2], ('replica', 'tp'), split_axis=0, concat_axis=0,...]
    all_to_all x3 -> x0, starting transfers between devices: 9.48 us -> none  [the longest x1 3.62 us: shards(): lax.all_to_all(shaped[1], ('replica', 'tp'), split_axis=0, concat_axis=0,...]
    reduce_sum x3 -> x0, other arithmetic: 4.34 us -> none  [the longest x1 4.26 us: shards(): jnp.sum(jnp.where(columns[None, :] == token_ids[:, None], logits, 0.0), a...]
    all_to_all x3 -> x0, local copies, waits for them, and re-layouts: 2.06 us -> none  [the longest x1 0.69 us: shards(): lax.all_to_all(shaped[2], ('replica', 'tp'), split_axis=0, concat_axis=0,...]
  transfers between devices with their start and end apart: 4 -> 0, of which waited for: 4 -> 0; matrix products, arithmetic and copies ran while one was open for 3% -> 0% of each run, Pallas kernels for 0% -> 0%
where the time goes in v1:
time: 72.7 us; the launch traced here: 72.5 us
  Pallas kernels  71.2 us (98%)
  local copies, waits for them, and re-layouts  1.31 us (2%)
    pallas_call x1, Pallas kernels, shards(): pl.pallas_call(functools.partial(kernel, dims, rows, slots), out_shape=ja...  71.2 us

profile of v1, /device:TPU:0, one launch (start us, length us, event | category | flops | bytes accessed | tf_op | source)
XLA Modules:
  0.0 72.5 jit_solution(17236863449492968058)
XLA Ops:
  0.0 71.2 %shard_map.37 = f32[8,128]{1,0:T(8,128)} custom-call(s32[1,256]{1,0:T(1,128)} %bitcast.1, bf16[8,8192]{1,0:T(8,128)(2,1)} %hidden_ref.1, bf16[4752,8192]{1,0:T(8,128)(2,1)} %head_ref.1), custom_call_target="tpu_custom_call" | custom-call | tf_op jit(solution)/shard_map/pallas_call | solution.py:208
  71.2 1.3 %slice_reduce_fusion = f32[8]{0:T(128)} fusion(f32[8,128]{1,0:T(8,128)} %shard_map.37), kind=kLoop, calls=%fused_computation | loop fusion | bytes 64 | tf_op jit(solution)/shard_map/slice | solution.py:232
